TPU v7x, 32 devices: a whole 2x2x4 slice. The times are simulated.
32 devices in a mesh: gx: 4 (over z), gy: 2 (over x), gz: 4 (over y, core).
Axes of the slice: x: 2, y: 2, z: 4, core: 2. Of those that a mesh axis runs over, the one named last changes fastest.
Arguments:
- old_slots: bfloat16 [4, 2, 32, 4096], P('gx', 'gy', 'gz'), may hold values from -6 to 6
- old_ids: int32 [4, 2, 32], P('gx', 'gy', 'gz'), may hold values from -1 to 31, as said below
- old_owner: int32 [4, 2, 32], P('gx', 'gy'), may hold values from 0 to 3, as said below
- coefficient: float32 [64, 32, 512], P('gx', 'gy', 'gz'), may hold values from 0.2 to 5
Outputs:
- solution: float32 [64, 32, 512], P('gx', 'gy', 'gz')
Inputs may be any that keep to these rules, and one draw needn't show every extreme that they name: old_owner[a, c, b] is the index along gz of the device that held box b of box column (a, c) before the move; no device holds more than 8 boxes of a column and some device holds exactly 8; no device holds more than 2 of the 8 boxes with one value of b // 8, and that bound is reached. old_ids[a, c, g * 8 + q] is the box held in slot q of device g of box column (a, c), or -1 for an empty slot; it agrees with old_owner and each box stands in exactly one slot.
All inputs are finite; a program needn't handle non-finite values.
Results may differ from a plain program's by a relative error of at most 0.0003.
Values may be sent and summed in bfloat16 or wider, within the bound.
No kernel may reach another device: no remote copies, remote signals or barrier semaphores. Data moves between devices by JAX's collectives and lax.ppermute only.
A program may use at most 64 MiB of HBM per device.

v0:
```python
import jax
import jax.numpy as jnp
from jax import lax
from jax.sharding import PartitionSpec as P

BOX = 16
NB = 8
SEND = 2
SWEEPS = 2


def with_halo(cells, sides, width):
    for axis, dim in sides:
        count = lax.axis_size(axis)
        ends = count - 1
        head = lax.slice_in_dim(cells, 0, width, axis=dim)
        tail = lax.slice_in_dim(cells, cells.shape[dim] - width, cells.shape[dim], axis=dim)
        cells = jnp.concatenate(
            [
                lax.ppermute(tail, axis, [(i, (i + 1) % count) for i in range(ends)]),
                cells,
                lax.ppermute(head, axis, [((i + 1) % count, i) for i in range(ends)]),
            ],
            axis=dim,
        )
    return cells


def rims(values, depth):
    return with_halo(values, (("gx", 0), ("gy", 1), ("gz", 2)), depth)


def inner(padded):
    return padded[1:-1, 1:-1, 1:-1]


def operator_parts(padded):
    face_first = 0.5 * (padded[:-1, 1:-1, 1:-1] + padded[1:, 1:-1, 1:-1])
    face_second = 0.5 * (padded[1:-1, :-1, 1:-1] + padded[1:-1, 1:, 1:-1])
    face_third = 0.5 * (padded[1:-1, 1:-1, :-1] + padded[1:-1, 1:-1, 1:])
    diagonal = (
        face_first[:-1]
        + face_first[1:]
        + face_second[:, :-1]
        + face_second[:, 1:]
        + face_third[:, :, :-1]
        + face_third[:, :, 1:]
    )
    return (face_first, face_second, face_third, diagonal)


def neighbours(padded, stencil):
    face_first, face_second, face_third, diagonal = stencil
    summed = face_first[:-1] * padded[:-2, 1:-1, 1:-1] + face_first[1:] * padded[2:, 1:-1, 1:-1]
    summed = (
        summed
        + face_second[:, :-1] * padded[1:-1, :-2, 1:-1]
        + face_second[:, 1:] * padded[1:-1, 2:, 1:-1]
    )
    summed = (
        summed
        + face_third[:, :, :-1] * padded[1:-1, 1:-1, :-2]
        + face_third[:, :, 1:] * padded[1:-1, 1:-1, 2:]
    )
    return summed


def red_cells(shape, margin):
    index_first = lax.broadcasted_iota(jnp.int32, shape, 0)
    index_second = lax.broadcasted_iota(jnp.int32, shape, 1)
    index_third = lax.broadcasted_iota(jnp.int32, shape, 2)
    return (index_first + index_second + index_third + margin) % 2 == 0


def relax(padded, source, stencil, factor, chosen):
    fresh = (factor * source + neighbours(padded, stencil)) / stencil[3]
    return jnp.where(chosen, fresh, inner(padded))


def apply_operator(values, stencil, factor):
    return (stencil[3] * values - neighbours(rims(values, 1), stencil)) / factor


def sweep_thin(values, source, stencil, factor, red_mask, starting):
    if starting:
        values = jnp.where(red_mask, factor * source / stencil[3], 0.0)
    else:
        values = relax(rims(values, 1), source, stencil, factor, red_mask)
    return relax(rims(values, 1), source, stencil, factor, jnp.logical_not(red_mask))


def smooth_thin(values, source, stencil, factor, starting):
    red_mask = red_cells(source.shape, 0)
    for counter in range(SWEEPS):
        values = sweep_thin(values, source, stencil, factor, red_mask, starting and counter == 0)
    return values


def sweep_deep(
    values, source_rim, stencil_rim, stencil_block, factor, red_rim, black_block, starting
):
    if starting:
        coloured = jnp.where(red_rim, factor * source_rim / stencil_rim[3], 0.0)
    else:
        coloured = relax(rims(values, 2), source_rim, stencil_rim, factor, red_rim)
    return relax(coloured, inner(source_rim), stencil_block, factor, black_block)


def coarsen(values):
    extent_first, extent_second, extent_third = values.shape
    grouped = values.reshape(extent_first // 2, 2, extent_second // 2, 2, extent_third // 2, 2)
    return grouped.mean(axis=(1, 3, 5))


def refine(values):
    return jnp.repeat(jnp.repeat(jnp.repeat(values, 2, axis=0), 2, axis=1), 2, axis=2)


def dot_pair(first_term, second_term):
    return lax.psum((first_term, second_term), ("gx", "gy", "gz"))


def bottom_solve(rhs_low, stencil, factor):
    image_low = apply_operator(rhs_low, stencil, factor)
    norm_rhs, along_rhs = dot_pair(jnp.sum(rhs_low * rhs_low), jnp.sum(rhs_low * image_low))
    alpha_step = norm_rhs / along_rhs
    rest_low = rhs_low - alpha_step * image_low
    turned = apply_operator(rest_low, stencil, factor)
    turned_rest, turned_norm = dot_pair(jnp.sum(turned * rest_low), jnp.sum(turned * turned))
    omega_step = turned_rest / turned_norm
    return alpha_step * rhs_low + omega_step * rest_low


def move_boxes(old_slots, old_ids, old_owner):
    slot_rows = old_slots.reshape(old_slots.shape[2], old_slots.shape[3])
    slot_ids = old_ids.reshape(-1)
    owner_map = old_owner.reshape(-1)
    groups = lax.axis_size("gz")
    my_index = lax.axis_index("gz")
    capacity = slot_ids.shape[0]
    filled = slot_ids >= 0
    target = jnp.where(filled, slot_ids // NB, -1)
    earlier = (
        (target[None, :] == target[:, None])
        & (slot_ids[None, :] < slot_ids[:, None])
        & filled[None, :]
    )
    ranking = jnp.sum(earlier.astype(jnp.int32), axis=1)
    send_row = jnp.where(filled, target * SEND + ranking, -1)
    picker = lax.broadcasted_iota(jnp.int32, (groups * SEND, capacity), 0) == send_row[None, :]
    outgoing = jnp.dot(
        picker.astype(jnp.bfloat16), slot_rows, preferred_element_type=jnp.float32
    ).astype(jnp.bfloat16)
    incoming = lax.all_to_all(outgoing, "gz", split_axis=0, concat_axis=0, tiled=True).astype(
        jnp.float32
    )
    arriving = lax.dynamic_slice_in_dim(owner_map, my_index * NB, NB)
    later_index = lax.broadcasted_iota(jnp.int32, (NB, NB), 0)
    before = (arriving[None, :] == arriving[:, None]) & (
        lax.broadcasted_iota(jnp.int32, (NB, NB), 1) < later_index
    )
    order_within = jnp.sum(before.astype(jnp.int32), axis=1)
    chosen_boxes = jnp.take(incoming, arriving * SEND + order_within, axis=0)
    stacked = chosen_boxes.reshape(NB, BOX, BOX, BOX).transpose(1, 2, 0, 3)
    return stacked.reshape(BOX, BOX, NB * BOX)


def per_device(old_slots, old_ids, old_owner, coefficient):
    source_fine = move_boxes(old_slots, old_ids, old_owner)
    coefficient_rim = rims(coefficient, 2)
    inside = inner(coefficient_rim) > 0.0
    face_first, face_second, face_third, diagonal = operator_parts(coefficient_rim)
    stencil_rim = (face_first, face_second, face_third, jnp.where(inside, diagonal, 1.0))
    stencil_fine = (inner(face_first), inner(face_second), inner(face_third), inner(diagonal))
    source_rim = rims(source_fine, 1)
    red_rim = jnp.logical_and(red_cells(inside.shape, 1), inside)
    black_fine = jnp.logical_not(red_cells(source_fine.shape, 0))

    def smooth_fine(values, starting):
        for counter in range(SWEEPS):
            values = sweep_deep(
                values,
                source_rim,
                stencil_rim,
                stencil_fine,
                1.0,
                red_rim,
                black_fine,
                starting and counter == 0,
            )
        return values

    fine_values = smooth_fine(jnp.zeros_like(source_fine), True)
    residual_fine = source_fine - apply_operator(fine_values, stencil_fine, 1.0)
    coefficient_mid = coarsen(coefficient)
    stencil_mid = operator_parts(rims(coefficient_mid, 1))
    source_mid = coarsen(residual_fine)
    middle_values = smooth_thin(jnp.zeros_like(source_mid), source_mid, stencil_mid, 4.0, True)
    residual_mid = source_mid - apply_operator(middle_values, stencil_mid, 4.0)
    coefficient_low = coarsen(coefficient_mid)
    stencil_low = operator_parts(rims(coefficient_low, 1))
    bottom_values = bottom_solve(coarsen(residual_mid), stencil_low, 16.0)
    middle_values = smooth_thin(
        middle_values + refine(bottom_values), source_mid, stencil_mid, 4.0, False
    )
    return smooth_fine(fine_values + refine(middle_values), False)


def solution(mesh):
    in_specs = (
        P("gx", "gy", "gz", None),
        P("gx", "gy", "gz"),
        P("gx", "gy", None),
        P("gx", "gy", "gz"),
    )
    out_specs = P("gx", "gy", "gz")
    return jax.shard_map(
        per_device, mesh=mesh, in_specs=in_specs, out_specs=out_specs, check_vma=False
    )
```

profile of v0, /device:TPU:1, one launch (start us, length us, event | category | flops | bytes accessed | tf_op | source)
XLA Modules:
  0.0 550.7 jit_solution(12764030653669933789)
XLA Ops:
  2.1 4.6 collective-permute-start
  10.5 4.2 all-to-all-start
  14.7 10.6 %reshape.184 = f32[8,2,8,2,64,2]{5,4,3,2,1,0:T(8,128)} reshape(f32[16,16,128]{2,1,0:T(8,128)} %param.7) | data formatting | bytes 262144 | tf_op jit(solution)/shard_map/reshape | solution.py:111
  25.3 4.0 reduce_sum.96
  29.9 4.2 collective-permute-start.24
  43.7 5.3 collective-permute-start.4
  52.1 4.4 collective-permute-done.5
  58.6 4.3 collective-permute-start.6
  73.9 4.6 collective-permute-start.10
  81.4 4.4 collective-permute-done.11
  94.6 4.0 collective-permute-start.14
  103.3 4.0 collective-permute-start.16
  110.4 4.4 collective-permute-done.17
  117.0 4.3 collective-permute-start.18
  133.0 4.7 collective-permute-start.22
  140.5 4.4 collective-permute-done.23
  145.4 9.8 %reshape.183 = f32[8,2,8,2,64,2]{5,4,3,2,1,0:T(8,128)} reshape(f32[16,16,128]{2,1,0:T(8,128)S(1)} %fusion.55) | data formatting | bytes 262144 | tf_op jit(solution)/shard_map/reshape | solution.py:111
  155.2 4.0 reduce_sum.95
  159.4 4.3 collective-permute-start.30
  173.9 4.6 collective-permute-start.34
  180.4 3.8 collective-permute-done.35
  196.8 4.7 collective-permute-start.40
  203.5 3.8 collective-permute-done.41
  219.3 4.7 collective-permute-start.46
  237.6 3.7 collective-permute-start.50
  245.8 6.5 %collective-permute-start.52 = (f32[10,10,1]{2,1,0:T(8,128)S(1)}, f32[10,10,1]{2,1,0:T(8,128)S(1)}, u32[]{:S(2)}, u32[]{:S(2)}) collective-permute-start(f32[10,10,1]{2,1,0:T(8,128)S(1)} %get-tuple-element.61), channel_id=1, source_target_pairs={{0,1},{1,2},{2,3},{4,5},{5,6},{6,7},{8,9},{9,10},{10,11},{12,13},{... | collective-permute-start | bytes 1208 | tf_op jit(solution)/shard_map/ppermute | solution.py:20
  254.2 3.8 collective-permute-done.53
  259.4 4.3 collective-permute-start.60
  275.2 4.8 collective-permute-start.64
  285.9 37.9 %all-reduce.1 = (f32[]{:T(128)}, f32[]{:T(128)}) all-reduce(f32[]{:T(128)} %get-tuple-element.8, f32[]{:T(128)} %get-tuple-element.7), channel_id=1, replica_groups=mesh['gx'=4,'gy'=2,'gz'=4] {'gx','gy','gz'}, use_global_device_ids=true, to_apply=%region_6.7 | all-reduce | flops 2 | bytes 16 | tf_op jit(solution)/shard_map/psum | solution.py:120
  331.1 4.3 collective-permute-start.68
  339.9 7.3 %collective-permute-start.70 = (f32[6,6,1]{2,1,0:T(8,128)S(1)}, f32[6,6,1]{2,1,0:T(8,128)S(1)}, u32[]{:S(2)}, u32[]{:S(2)}) collective-permute-start(f32[6,6,1]{2,1,0:T(8,128)S(1)} %get-tuple-element.107), channel_id=1, source_target_pairs={{0,1},{1,2},{2,3},{4,5},{5,6},{6,7},{8,9},{9,10},{10,11},{12,13},{... | collective-permute-start | bytes 440 | tf_op jit(solution)/shard_map/ppermute | solution.py:20
  353.2 36.6 %all-reduce = (f32[]{:T(128)}, f32[]{:T(128)}) all-reduce(f32[]{:T(128)} %get-tuple-element.6, f32[]{:T(128)} %get-tuple-element.5), channel_id=1, replica_groups=mesh['gx'=4,'gy'=2,'gz'=4] {'gx','gy','gz'}, use_global_device_ids=true, to_apply=%region_11.12 | all-reduce | flops 2 | bytes 16 | tf_op jit(solution)/shard_map/psum | solution.py:120
  398.2 4.3 collective-permute-start.74
  407.0 7.3 %collective-permute-start.76 = (f32[10,10,1]{2,1,0:T(8,128)S(1)}, f32[10,10,1]{2,1,0:T(8,128)S(1)}, u32[]{:S(2)}, u32[]{:S(2)}) collective-permute-start(f32[10,10,1]{2,1,0:T(8,128)S(1)} %get-tuple-element.59), channel_id=1, source_target_pairs={{0,1},{1,2},{2,3},{4,5},{5,6},{6,7},{8,9},{9,10},{10,11},{12,13},{... | collective-permute-start | bytes 1208 | tf_op jit(solution)/shard_map/ppermute | solution.py:20
  416.3 3.8 collective-permute-done.77
  423.9 3.3 collective-permute-done.79
  433.1 4.4 collective-permute-start.82
  439.5 3.8 collective-permute-done.83
  443.4 3.6 collective-permute-start.84
  457.3 4.7 collective-permute-start.88
  464.0 3.8 collective-permute-done.89
  479.8 4.7 collective-permute-start.94
  486.7 3.6 collective-permute-done.95
  507.0 4.7 collective-permute-start.100
  514.8 4.4 collective-permute-done.101
  534.7 4.6 collective-permute-start.106
  542.4 4.4 collective-permute-done.107
  (362 shorter events, 254.7 us)
Async XLA Ops:
  0.8 35.1 %collective-permute-start.1 = (f32[2,16,128]{2,1,0:T(8,128)S(1)}, f32[2,16,128]{2,1,0:T(8,128)S(1)}, u32[]{:S(2)}, u32[]{:S(2)}) collective-permute-start(f32[2,16,128]{2,1,0:T(8,128)S(1)} %get-tuple-element.51), channel_id=1, source_target_pairs={{8,0},{16,8},{24,16},{9,1},{17,9},{25,17},{10,2},{18,10},{26,18},{... | collective-permute-start | bytes 49160 | tf_op jit(solution)/shard_map/ppermute | solution.py:22
  2.1 33.7 %collective-permute-start = (f32[2,16,128]{2,1,0:T(8,128)S(1)}, f32[2,16,128]{2,1,0:T(8,128)S(1)}, u32[]{:S(2)}, u32[]{:S(2)}) collective-permute-start(f32[2,16,128]{2,1,0:T(8,128)S(1)} %get-tuple-element.52), channel_id=1, source_target_pairs={{0,8},{8,16},{16,24},{1,9},{9,17},{17,25},{2,10},{10,18},{18,26},{... | collective-permute-start | bytes 49160 | tf_op jit(solution)/shard_map/ppermute | solution.py:20
  10.5 46.4 %all-to-all-start = ((bf16[4,2,4096]{2,1,0:T(2,128)(2,1)}), bf16[4,2,4096]{2,1,0:T(2,128)(2,1)S(1)}, u32[]{:S(2)}, u32[]{:S(2)}) async-start(bf16[4,2,4096]{2,1,0:T(2,128)(2,1)} %all_to_all.6), calls=%async_computation | async-start | bytes 131072 | tf_op jit(solution)/shard_map/all_to_all | solution.py:154
  29.9 61.0 %collective-permute-start.24 = (f32[1,8,64]{2,1,0:T(8,128)}, f32[1,8,64]{2,1,0:T(8,128)}, u32[]{:S(2)}, u32[]{:S(2)}) collective-permute-start(f32[1,8,64]{2,1,0:T(8,128)} %get-tuple-element.105), channel_id=1, source_target_pairs={{0,8},{8,16},{16,24},{1,9},{9,17},{17,25},{2,10},{10,18},{18,26},{... | collective-permute-start | bytes 6152 | tf_op jit(solution)/shard_map/ppermute | solution.py:20
  34.2 56.8 %collective-permute-start.25 = (f32[1,8,64]{2,1,0:T(8,128)}, f32[1,8,64]{2,1,0:T(8,128)}, u32[]{:S(2)}, u32[]{:S(2)}) collective-permute-start(f32[1,8,64]{2,1,0:T(8,128)} %get-tuple-element.106), channel_id=1, source_target_pairs={{8,0},{16,8},{24,16},{9,1},{17,9},{25,17},{10,2},{18,10},{26,18},{... | collective-permute-start | bytes 6152 | tf_op jit(solution)/shard_map/ppermute | solution.py:22
  43.7 8.4 %collective-permute-start.4 = (f32[20,20,2]{2,1,0:T(8,128)S(1)}, f32[20,20,2]{2,1,0:T(8,128)S(1)}, u32[]{:S(2)}, u32[]{:S(2)}) collective-permute-start(f32[20,20,2]{2,1,0:T(8,128)S(1)} %get-tuple-element.25), channel_id=1, source_target_pairs={{0,1},{1,2},{2,3},{4,5},{5,6},{6,7},{8,9},{9,10},{10,11},{12,13},{... | collective-permute-start | bytes 9608 | tf_op jit(solution)/shard_map/ppermute | solution.py:20
  49.0 7.5 %collective-permute-start.5 = (f32[20,20,2]{2,1,0:T(8,128)S(1)}, f32[20,20,2]{2,1,0:T(8,128)S(1)}, u32[]{:S(2)}, u32[]{:S(2)}) collective-permute-start(f32[20,20,2]{2,1,0:T(8,128)S(1)} %get-tuple-element.26), channel_id=1, source_target_pairs={{1,0},{2,1},{3,2},{5,4},{6,5},{7,6},{9,8},{10,9},{11,10},{13,12},{... | collective-permute-start | bytes 9608 | tf_op jit(solution)/shard_map/ppermute | solution.py:22
  58.6 6.3 %collective-permute-start.6 = (f32[1,16,128]{2,1,0:T(8,128)S(1)}, f32[1,16,128]{2,1,0:T(8,128)S(1)}, u32[]{:S(2)}, u32[]{:S(2)}) collective-permute-start(f32[1,16,128]{2,1,0:T(8,128)S(1)} %slice.1002), channel_id=1, source_target_pairs={{0,8},{8,16},{16,24},{1,9},{9,17},{17,25},{2,10},{10,18},{18,26},{... | collective-permute-start | bytes 24584 | tf_op jit(solution)/shard_map/ppermute | solution.py:20
  73.9 7.5 %collective-permute-start.10 = (f32[18,18,1]{2,1,0:T(8,128)S(1)}, f32[18,18,1]{2,1,0:T(8,128)S(1)}, u32[]{:S(2)}, u32[]{:S(2)}) collective-permute-start(f32[18,18,1]{2,1,0:T(8,128)S(1)} %get-tuple-element.29), channel_id=1, source_target_pairs={{0,1},{1,2},{2,3},{4,5},{5,6},{6,7},{8,9},{9,10},{10,11},{12,13},{... | collective-permute-start | bytes 3896 | tf_op jit(solution)/shard_map/ppermute | solution.py:20
  78.5 7.3 %collective-permute-start.11 = (f32[18,18,1]{2,1,0:T(8,128)S(1)}, f32[18,18,1]{2,1,0:T(8,128)S(1)}, u32[]{:S(2)}, u32[]{:S(2)}) collective-permute-start(f32[18,18,1]{2,1,0:T(8,128)S(1)} %get-tuple-element.30), channel_id=1, source_target_pairs={{1,0},{2,1},{3,2},{5,4},{6,5},{7,6},{9,8},{10,9},{11,10},{13,12},{... | collective-permute-start | bytes 3896 | tf_op jit(solution)/shard_map/ppermute | solution.py:22
  87.0 7.5 %collective-permute-start.12 = (f32[2,16,128]{2,1,0:T(8,128)S(1)}, f32[2,16,128]{2,1,0:T(8,128)S(1)}, u32[]{:S(2)}, u32[]{:S(2)}) collective-permute-start(f32[2,16,128]{2,1,0:T(8,128)S(1)} %get-tuple-element.49), channel_id=1, source_target_pairs={{0,8},{8,16},{16,24},{1,9},{9,17},{17,25},{2,10},{10,18},{18,26},{... | collective-permute-start | bytes 49160 | tf_op jit(solution)/shard_map/ppermute | solution.py:20
  91.9 17.4 %collective-permute-start.26 = (f32[10,1,64]{2,1,0:T(1,128)S(1)}, f32[10,1,64]{2,1,0:T(1,128)S(1)}, u32[]{:S(2)}, u32[]{:S(2)}) collective-permute-start(f32[10,1,64]{2,1,0:T(1,128)S(1)} %get-tuple-element.87), channel_id=1, source_target_pairs={{0,4},{1,5},{2,6},{3,7},{8,12},{9,13},{10,14},{11,15},{16,20},{17,... | collective-permute-start | bytes 7688 | tf_op jit(solution)/shard_map/ppermute | solution.py:20
  93.2 16.0 %collective-permute-start.27 = (f32[10,1,64]{2,1,0:T(1,128)S(1)}, f32[10,1,64]{2,1,0:T(1,128)S(1)}, u32[]{:S(2)}, u32[]{:S(2)}) collective-permute-start(f32[10,1,64]{2,1,0:T(1,128)S(1)} %get-tuple-element.88), channel_id=1, source_target_pairs={{4,0},{5,1},{6,2},{7,3},{12,8},{13,9},{14,10},{15,11},{20,16},{21,... | collective-permute-start | bytes 7688 | tf_op jit(solution)/shard_map/ppermute | solution.py:22
  94.6 6.1 %collective-permute-start.14 = (f32[20,2,128]{2,1,0:T(2,128)S(1)}, f32[20,2,128]{2,1,0:T(2,128)S(1)}, u32[]{:S(2)}, u32[]{:S(2)}) collective-permute-start(f32[20,2,128]{2,1,0:T(2,128)S(1)} %get-tuple-element.35), channel_id=1, source_target_pairs={{0,4},{1,5},{2,6},{3,7},{8,12},{9,13},{10,14},{11,15},{16,20},{17,... | collective-permute-start | bytes 61448 | tf_op jit(solution)/shard_map/ppermute | solution.py:20
  103.3 7.1 %collective-permute-start.16 = (f32[20,20,2]{2,1,0:T(8,128)S(1)}, f32[20,20,2]{2,1,0:T(8,128)S(1)}, u32[]{:S(2)}, u32[]{:S(2)}) collective-permute-start(f32[20,20,2]{2,1,0:T(8,128)S(1)} %get-tuple-element.23), channel_id=1, source_target_pairs={{0,1},{1,2},{2,3},{4,5},{5,6},{6,7},{8,9},{9,10},{10,11},{12,13},{... | collective-permute-start | bytes 9608 | tf_op jit(solution)/shard_map/ppermute | solution.py:20
  107.3 7.5 %collective-permute-start.17 = (f32[20,20,2]{2,1,0:T(8,128)S(1)}, f32[20,20,2]{2,1,0:T(8,128)S(1)}, u32[]{:S(2)}, u32[]{:S(2)}) collective-permute-start(f32[20,20,2]{2,1,0:T(8,128)S(1)} %get-tuple-element.24), channel_id=1, source_target_pairs={{1,0},{2,1},{3,2},{5,4},{6,5},{7,6},{9,8},{10,9},{11,10},{13,12},{... | collective-permute-start | bytes 9608 | tf_op jit(solution)/shard_map/ppermute | solution.py:22
  117.0 10.0 %collective-permute-start.18 = (f32[1,16,128]{2,1,0:T(8,128)S(1)}, f32[1,16,128]{2,1,0:T(8,128)S(1)}, u32[]{:S(2)}, u32[]{:S(2)}) collective-permute-start(f32[1,16,128]{2,1,0:T(8,128)S(1)} %get-tuple-element.47), channel_id=1, source_target_pairs={{0,8},{8,16},{16,24},{1,9},{9,17},{17,25},{2,10},{10,18},{18,26},{... | collective-permute-start | bytes 24584 | tf_op jit(solution)/shard_map/ppermute | solution.py:20
  122.7 17.1 %collective-permute-start.28 = (f32[10,10,1]{2,1,0:T(8,128)S(1)}, f32[10,10,1]{2,1,0:T(8,128)S(1)}, u32[]{:S(2)}, u32[]{:S(2)}) collective-permute-start(f32[10,10,1]{2,1,0:T(8,128)S(1)} %get-tuple-element.69), channel_id=1, source_target_pairs={{0,1},{1,2},{2,3},{4,5},{5,6},{6,7},{8,9},{9,10},{10,11},{12,13},{... | collective-permute-start | bytes 1208 | tf_op jit(solution)/shard_map/ppermute | solution.py:20
  124.7 15.1 %collective-permute-start.29 = (f32[10,10,1]{2,1,0:T(8,128)S(1)}, f32[10,10,1]{2,1,0:T(8,128)S(1)}, u32[]{:S(2)}, u32[]{:S(2)}) collective-permute-start(f32[10,10,1]{2,1,0:T(8,128)S(1)} %get-tuple-element.70), channel_id=1, source_target_pairs={{1,0},{2,1},{3,2},{5,4},{6,5},{7,6},{9,8},{10,9},{11,10},{13,12},{... | collective-permute-start | bytes 1208 | tf_op jit(solution)/shard_map/ppermute | solution.py:22
  133.0 7.6 %collective-permute-start.22 = (f32[18,18,1]{2,1,0:T(8,128)S(1)}, f32[18,18,1]{2,1,0:T(8,128)S(1)}, u32[]{:S(2)}, u32[]{:S(2)}) collective-permute-start(f32[18,18,1]{2,1,0:T(8,128)S(1)} %get-tuple-element.27), channel_id=1, source_target_pairs={{0,1},{1,2},{2,3},{4,5},{5,6},{6,7},{8,9},{9,10},{10,11},{12,13},{... | collective-permute-start | bytes 3896 | tf_op jit(solution)/shard_map/ppermute | solution.py:20
  137.7 7.3 %collective-permute-start.23 = (f32[18,18,1]{2,1,0:T(8,128)S(1)}, f32[18,18,1]{2,1,0:T(8,128)S(1)}, u32[]{:S(2)}, u32[]{:S(2)}) collective-permute-start(f32[18,18,1]{2,1,0:T(8,128)S(1)} %get-tuple-element.28), channel_id=1, source_target_pairs={{1,0},{2,1},{3,2},{5,4},{6,5},{7,6},{9,8},{10,9},{11,10},{13,12},{... | collective-permute-start | bytes 3896 | tf_op jit(solution)/shard_map/ppermute | solution.py:22
  173.9 6.5 %collective-permute-start.34 = (f32[10,10,1]{2,1,0:T(8,128)S(1)}, f32[10,10,1]{2,1,0:T(8,128)S(1)}, u32[]{:S(2)}, u32[]{:S(2)}) collective-permute-start(f32[10,10,1]{2,1,0:T(8,128)S(1)} %get-tuple-element.67), channel_id=1, source_target_pairs={{0,1},{1,2},{2,3},{4,5},{5,6},{6,7},{8,9},{9,10},{10,11},{12,13},{... | collective-permute-start | bytes 1208 | tf_op jit(solution)/shard_map/ppermute | solution.py:20
  178.5 5.8 %collective-permute-start.35 = (f32[10,10,1]{2,1,0:T(8,128)S(1)}, f32[10,10,1]{2,1,0:T(8,128)S(1)}, u32[]{:S(2)}, u32[]{:S(2)}) collective-permute-start(f32[10,10,1]{2,1,0:T(8,128)S(1)} %get-tuple-element.68), channel_id=1, source_target_pairs={{1,0},{2,1},{3,2},{5,4},{6,5},{7,6},{9,8},{10,9},{11,10},{13,12},{... | collective-permute-start | bytes 1208 | tf_op jit(solution)/shard_map/ppermute | solution.py:22
  196.8 6.6 %collective-permute-start.40 = (f32[10,10,1]{2,1,0:T(8,128)S(1)}, f32[10,10,1]{2,1,0:T(8,128)S(1)}, u32[]{:S(2)}, u32[]{:S(2)}) collective-permute-start(f32[10,10,1]{2,1,0:T(8,128)S(1)} %get-tuple-element.65), channel_id=1, source_target_pairs={{0,1},{1,2},{2,3},{4,5},{5,6},{6,7},{8,9},{9,10},{10,11},{12,13},{... | collective-permute-start | bytes 1208 | tf_op jit(solution)/shard_map/ppermute | solution.py:20
  201.5 5.8 %collective-permute-start.41 = (f32[10,10,1]{2,1,0:T(8,128)S(1)}, f32[10,10,1]{2,1,0:T(8,128)S(1)}, u32[]{:S(2)}, u32[]{:S(2)}) collective-permute-start(f32[10,10,1]{2,1,0:T(8,128)S(1)} %get-tuple-element.66), channel_id=1, source_target_pairs={{1,0},{2,1},{3,2},{5,4},{6,5},{7,6},{9,8},{10,9},{11,10},{13,12},{... | collective-permute-start | bytes 1208 | tf_op jit(solution)/shard_map/ppermute | solution.py:22
  219.3 9.7 %collective-permute-start.46 = (f32[10,10,1]{2,1,0:T(8,128)S(1)}, f32[10,10,1]{2,1,0:T(8,128)S(1)}, u32[]{:S(2)}, u32[]{:S(2)}) collective-permute-start(f32[10,10,1]{2,1,0:T(8,128)S(1)} %get-tuple-element.63), channel_id=1, source_target_pairs={{0,1},{1,2},{2,3},{4,5},{5,6},{6,7},{8,9},{9,10},{10,11},{12,13},{... | collective-permute-start | bytes 1208 | tf_op jit(solution)/shard_map/ppermute | solution.py:20
  224.0 5.8 %collective-permute-start.47 = (f32[10,10,1]{2,1,0:T(8,128)S(1)}, f32[10,10,1]{2,1,0:T(8,128)S(1)}, u32[]{:S(2)}, u32[]{:S(2)}) collective-permute-start(f32[10,10,1]{2,1,0:T(8,128)S(1)} %get-tuple-element.64), channel_id=1, source_target_pairs={{1,0},{2,1},{3,2},{5,4},{6,5},{7,6},{9,8},{10,9},{11,10},{13,12},{... | collective-permute-start | bytes 1208 | tf_op jit(solution)/shard_map/ppermute | solution.py:22
  226.0 8.6 %collective-permute-start.54 = (f32[1,4,32]{2,1,0:T(4,128)S(1)}, f32[1,4,32]{2,1,0:T(4,128)S(1)}, u32[]{:S(2)}, u32[]{:S(2)}) collective-permute-start(f32[1,4,32]{2,1,0:T(4,128)S(1)} %get-tuple-element.121), channel_id=1, source_target_pairs={{0,8},{8,16},{16,24},{1,9},{9,17},{17,25},{2,10},{10,18},{18,26},{... | collective-permute-start | bytes 1544 | tf_op jit(solution)/shard_map/ppermute | solution.py:20
  227.6 6.9 %collective-permute-start.55 = (f32[1,4,32]{2,1,0:T(4,128)S(1)}, f32[1,4,32]{2,1,0:T(4,128)S(1)}, u32[]{:S(2)}, u32[]{:S(2)}) collective-permute-start(f32[1,4,32]{2,1,0:T(4,128)S(1)} %get-tuple-element.122), channel_id=1, source_target_pairs={{8,0},{16,8},{24,16},{9,1},{17,9},{25,17},{10,2},{18,10},{26,18},{... | collective-permute-start | bytes 1544 | tf_op jit(solution)/shard_map/ppermute | solution.py:22
  229.9 7.3 %collective-permute-start.48 = (f32[1,8,64]{2,1,0:T(8,128)S(1)}, f32[1,8,64]{2,1,0:T(8,128)S(1)}, u32[]{:S(2)}, u32[]{:S(2)}) collective-permute-start(f32[1,8,64]{2,1,0:T(8,128)S(1)} %get-tuple-element.97), channel_id=1, source_target_pairs={{0,8},{8,16},{16,24},{1,9},{9,17},{17,25},{2,10},{10,18},{18,26},{... | collective-permute-start | bytes 6152 | tf_op jit(solution)/shard_map/ppermute | solution.py:20
  234.6 19.6 %collective-permute-start.56 = (f32[6,1,32]{2,1,0:T(1,128)S(1)}, f32[6,1,32]{2,1,0:T(1,128)S(1)}, u32[]{:S(2)}, u32[]{:S(2)}) collective-permute-start(f32[6,1,32]{2,1,0:T(1,128)S(1)} %get-tuple-element.115), channel_id=1, source_target_pairs={{0,4},{1,5},{2,6},{3,7},{8,12},{9,13},{10,14},{11,15},{16,20},{17,... | collective-permute-start | bytes 2312 | tf_op jit(solution)/shard_map/ppermute | solution.py:20
  235.9 18.2 %collective-permute-start.57 = (f32[6,1,32]{2,1,0:T(1,128)S(1)}, f32[6,1,32]{2,1,0:T(1,128)S(1)}, u32[]{:S(2)}, u32[]{:S(2)}) collective-permute-start(f32[6,1,32]{2,1,0:T(1,128)S(1)} %get-tuple-element.116), channel_id=1, source_target_pairs={{4,0},{5,1},{6,2},{7,3},{12,8},{13,9},{14,10},{15,11},{20,16},{21,... | collective-permute-start | bytes 2312 | tf_op jit(solution)/shard_map/ppermute | solution.py:22
  245.8 8.5 %collective-permute-start.52 = (f32[10,10,1]{2,1,0:T(8,128)S(1)}, f32[10,10,1]{2,1,0:T(8,128)S(1)}, u32[]{:S(2)}, u32[]{:S(2)}) collective-permute-start(f32[10,10,1]{2,1,0:T(8,128)S(1)} %get-tuple-element.61), channel_id=1, source_target_pairs={{0,1},{1,2},{2,3},{4,5},{5,6},{6,7},{8,9},{9,10},{10,11},{12,13},{... | collective-permute-start | bytes 1208 | tf_op jit(solution)/shard_map/ppermute | solution.py:20
  252.2 5.8 %collective-permute-start.53 = (f32[10,10,1]{2,1,0:T(8,128)S(1)}, f32[10,10,1]{2,1,0:T(8,128)S(1)}, u32[]{:S(2)}, u32[]{:S(2)}) collective-permute-start(f32[10,10,1]{2,1,0:T(8,128)S(1)} %get-tuple-element.62), channel_id=1, source_target_pairs={{1,0},{2,1},{3,2},{5,4},{6,5},{7,6},{9,8},{10,9},{11,10},{13,12},{... | collective-permute-start | bytes 1208 | tf_op jit(solution)/shard_map/ppermute | solution.py:22
  259.4 10.0 %collective-permute-start.60 = (f32[1,4,32]{2,1,0:T(4,128)S(1)}, f32[1,4,32]{2,1,0:T(4,128)S(1)}, u32[]{:S(2)}, u32[]{:S(2)}) collective-permute-start(f32[1,4,32]{2,1,0:T(4,128)S(1)} %get-tuple-element.123), channel_id=1, source_target_pairs={{0,8},{8,16},{16,24},{1,9},{9,17},{17,25},{2,10},{10,18},{18,26},{... | collective-permute-start | bytes 1544 | tf_op jit(solution)/shard_map/ppermute | solution.py:20
  265.0 16.9 %collective-permute-start.58 = (f32[6,6,1]{2,1,0:T(8,128)S(1)}, f32[6,6,1]{2,1,0:T(8,128)S(1)}, u32[]{:S(2)}, u32[]{:S(2)}) collective-permute-start(f32[6,6,1]{2,1,0:T(8,128)S(1)} %get-tuple-element.109), channel_id=1, source_target_pairs={{0,1},{1,2},{2,3},{4,5},{5,6},{6,7},{8,9},{9,10},{10,11},{12,13},{... | collective-permute-start | bytes 440 | tf_op jit(solution)/shard_map/ppermute | solution.py:20
  267.2 14.8 %collective-permute-start.59 = (f32[6,6,1]{2,1,0:T(8,128)S(1)}, f32[6,6,1]{2,1,0:T(8,128)S(1)}, u32[]{:S(2)}, u32[]{:S(2)}) collective-permute-start(f32[6,6,1]{2,1,0:T(8,128)S(1)} %get-tuple-element.110), channel_id=1, source_target_pairs={{1,0},{2,1},{3,2},{5,4},{6,5},{7,6},{9,8},{10,9},{11,10},{13,12},{... | collective-permute-start | bytes 440 | tf_op jit(solution)/shard_map/ppermute | solution.py:22
  275.2 7.6 %collective-permute-start.64 = (f32[6,6,1]{2,1,0:T(8,128)S(1)}, f32[6,6,1]{2,1,0:T(8,128)S(1)}, u32[]{:S(2)}, u32[]{:S(2)}) collective-permute-start(f32[6,6,1]{2,1,0:T(8,128)S(1)} %get-tuple-element.111), channel_id=1, source_target_pairs={{0,1},{1,2},{2,3},{4,5},{5,6},{6,7},{8,9},{9,10},{10,11},{12,13},{... | collective-permute-start | bytes 440 | tf_op jit(solution)/shard_map/ppermute | solution.py:20
  339.9 9.3 %collective-permute-start.70 = (f32[6,6,1]{2,1,0:T(8,128)S(1)}, f32[6,6,1]{2,1,0:T(8,128)S(1)}, u32[]{:S(2)}, u32[]{:S(2)}) collective-permute-start(f32[6,6,1]{2,1,0:T(8,128)S(1)} %get-tuple-element.107), channel_id=1, source_target_pairs={{0,1},{1,2},{2,3},{4,5},{5,6},{6,7},{8,9},{9,10},{10,11},{12,13},{... | collective-permute-start | bytes 440 | tf_op jit(solution)/shard_map/ppermute | solution.py:20
  407.0 9.3 %collective-permute-start.76 = (f32[10,10,1]{2,1,0:T(8,128)S(1)}, f32[10,10,1]{2,1,0:T(8,128)S(1)}, u32[]{:S(2)}, u32[]{:S(2)}) collective-permute-start(f32[10,10,1]{2,1,0:T(8,128)S(1)} %get-tuple-element.59), channel_id=1, source_target_pairs={{0,1},{1,2},{2,3},{4,5},{5,6},{6,7},{8,9},{9,10},{10,11},{12,13},{... | collective-permute-start | bytes 1208 | tf_op jit(solution)/shard_map/ppermute | solution.py:20
  414.3 5.8 %collective-permute-start.77 = (f32[10,10,1]{2,1,0:T(8,128)S(1)}, f32[10,10,1]{2,1,0:T(8,128)S(1)}, u32[]{:S(2)}, u32[]{:S(2)}) collective-permute-start(f32[10,10,1]{2,1,0:T(8,128)S(1)} %get-tuple-element.60), channel_id=1, source_target_pairs={{1,0},{2,1},{3,2},{5,4},{6,5},{7,6},{9,8},{10,9},{11,10},{13,12},{... | collective-permute-start | bytes 1208 | tf_op jit(solution)/shard_map/ppermute | solution.py:22
  433.1 6.4 %collective-permute-start.82 = (f32[10,10,1]{2,1,0:T(8,128)S(1)}, f32[10,10,1]{2,1,0:T(8,128)S(1)}, u32[]{:S(2)}, u32[]{:S(2)}) collective-permute-start(f32[10,10,1]{2,1,0:T(8,128)S(1)} %get-tuple-element.57), channel_id=1, source_target_pairs={{0,1},{1,2},{2,3},{4,5},{5,6},{6,7},{8,9},{9,10},{10,11},{12,13},{... | collective-permute-start | bytes 1208 | tf_op jit(solution)/shard_map/ppermute | solution.py:20
  457.3 6.6 %collective-permute-start.88 = (f32[10,10,1]{2,1,0:T(8,128)S(1)}, f32[10,10,1]{2,1,0:T(8,128)S(1)}, u32[]{:S(2)}, u32[]{:S(2)}) collective-permute-start(f32[10,10,1]{2,1,0:T(8,128)S(1)} %get-tuple-element.55), channel_id=1, source_target_pairs={{0,1},{1,2},{2,3},{4,5},{5,6},{6,7},{8,9},{9,10},{10,11},{12,13},{... | collective-permute-start | bytes 1208 | tf_op jit(solution)/shard_map/ppermute | solution.py:20
  479.8 6.9 %collective-permute-start.94 = (f32[10,10,1]{2,1,0:T(8,128)S(1)}, f32[10,10,1]{2,1,0:T(8,128)S(1)}, u32[]{:S(2)}, u32[]{:S(2)}) collective-permute-start(f32[10,10,1]{2,1,0:T(8,128)S(1)} %get-tuple-element.53), channel_id=1, source_target_pairs={{0,1},{1,2},{2,3},{4,5},{5,6},{6,7},{8,9},{9,10},{10,11},{12,13},{... | collective-permute-start | bytes 1208 | tf_op jit(solution)/shard_map/ppermute | solution.py:20
  507.0 7.8 %collective-permute-start.100 = (f32[20,20,2]{2,1,0:T(8,128)S(1)}, f32[20,20,2]{2,1,0:T(8,128)S(1)}, u32[]{:S(2)}, u32[]{:S(2)}) collective-permute-start(f32[20,20,2]{2,1,0:T(8,128)S(1)} %get-tuple-element.21), channel_id=1, source_target_pairs={{0,1},{1,2},{2,3},{4,5},{5,6},{6,7},{8,9},{9,10},{10,11},{12,13},{... | collective-permute-start | bytes 9608 | tf_op jit(solution)/shard_map/ppermute | solution.py:20
  511.7 7.5 %collective-permute-start.101 = (f32[20,20,2]{2,1,0:T(8,128)S(1)}, f32[20,20,2]{2,1,0:T(8,128)S(1)}, u32[]{:S(2)}, u32[]{:S(2)}) collective-permute-start(f32[20,20,2]{2,1,0:T(8,128)S(1)} %get-tuple-element.22), channel_id=1, source_target_pairs={{1,0},{2,1},{3,2},{5,4},{6,5},{7,6},{9,8},{10,9},{11,10},{13,12},{... | collective-permute-start | bytes 9608 | tf_op jit(solution)/shard_map/ppermute | solution.py:22
  534.7 7.7 %collective-permute-start.106 = (f32[20,20,2]{2,1,0:T(8,128)S(1)}, f32[20,20,2]{2,1,0:T(8,128)S(1)}, u32[]{:S(2)}, u32[]{:S(2)}) collective-permute-start(f32[20,20,2]{2,1,0:T(8,128)S(1)} %get-tuple-element.19), channel_id=1, source_target_pairs={{0,1},{1,2},{2,3},{4,5},{5,6},{6,7},{8,9},{9,10},{10,11},{12,13},{... | collective-permute-start | bytes 9608 | tf_op jit(solution)/shard_map/ppermute | solution.py:20
  539.3 7.5 %collective-permute-start.107 = (f32[20,20,2]{2,1,0:T(8,128)S(1)}, f32[20,20,2]{2,1,0:T(8,128)S(1)}, u32[]{:S(2)}, u32[]{:S(2)}) collective-permute-start(f32[20,20,2]{2,1,0:T(8,128)S(1)} %get-tuple-element.20), channel_id=1, source_target_pairs={{1,0},{2,1},{3,2},{5,4},{6,5},{7,6},{9,8},{10,9},{11,10},{13,12},{... | collective-permute-start | bytes 9608 | tf_op jit(solution)/shard_map/ppermute | solution.py:22
  (78 other events, 1132.2 us)
where the time goes:
time: 554 us; the launch traced here: 551 us
  starting transfers between devices  262 us (47%)
  waiting for transfers between devices  145 us (26%)
  blocking collectives  74.6 us (13%)
  other arithmetic  32.8 us (6%)
  local copies, waits for them, and re-layouts  31.5 us (6%)
    ppermute x54, starting transfers between devices, with_halo(): lax.ppermute(tail, axis, [(i, (i + 1) % count) for i in range(ends)])  175 us
    ppermute x54, waiting for transfers between devices, with_halo(): lax.ppermute(head, axis, [((i + 1) % count, i) for i in range(ends)])  140 us
    ppermute x54, starting transfers between devices, with_halo(): lax.ppermute(head, axis, [((i + 1) % count, i) for i in range(ends)])  82.2 us
    psum x2, blocking collectives, dot_pair(): return lax.psum((first_term, second_term), ('gx', 'gy', 'gz'))  74.6 us
    reshape x3, local copies, waits for them, and re-layouts, coarsen(): values.reshape(extent_first // 2, 2, extent_second // 2, 2, extent_third...  21.5 us
  transfers between devices with their start and end apart: 109, of which 50 were waited for; matrix products, arithmetic and copies ran while one was open for 5% of the time, Pallas kernels for 0%

commit v1 on v0

--- a/solution.py
+++ b/solution.py
@@ -117,7 +117,7 @@
 
 
 def dot_pair(first_term, second_term):
-    return lax.psum((first_term, second_term), ("gx", "gy", "gz"))
+    return lax.psum(lax.psum((first_term, second_term), ("gy", "gz")), "gx")
 
 
 def bottom_solve(rhs_low, stencil, factor):

time: 554 us -> 513 us (0.926)
  blocking collectives: 74.6 us -> 38 us
    psum x2 -> x4, blocking collectives: 74.6 us -> 38 us  [dot_pair(): return lax.psum(lax.psum((first_term, second_term), ('gy', 'gz')), 'gx')]
  transfers between devices with their start and end apart: 109 -> 109, of which waited for: 50 -> 50; matrix products, arithmetic and copies ran while one was open for 5% -> 6% of each run, Pallas kernels for 0% -> 0%
where the time goes in v1:
time: 513 us; the launch traced here: 510 us
  starting transfers between devices  258 us (50%)
  waiting for transfers between devices  145 us (28%)
  blocking collectives  38 us (7%)
  other arithmetic  32.9 us (6%)
  local copies, waits for them, and re-layouts  31.6 us (6%)
    ppermute x54, starting transfers between devices, with_halo(): lax.ppermute(tail, axis, [(i, (i + 1) % count) for i in range(ends)])  171 us
    ppermute x54, waiting for transfers between devices, with_halo(): lax.ppermute(head, axis, [((i + 1) % count, i) for i in range(ends)])  139 us
    ppermute x54, starting transfers between devices, with_halo(): lax.ppermute(head, axis, [((i + 1) % count, i) for i in range(ends)])  82.3 us
    psum x4, blocking collectives, dot_pair(): return lax.psum(lax.psum((first_term, second_term), ('gy', 'gz')), 'gx')  38 us
    reshape x3, local copies, waits for them, and re-layouts, coarsen(): values.reshape(extent_first // 2, 2, extent_second // 2, 2, extent_third...  21.5 us
  transfers between devices with their start and end apart: 109, of which 50 were waited for; matrix products, arithmetic and copies ran while one was open for 6% of the time, Pallas kernels for 0%

profile of v1, /device:TPU:1, one launch (start us, length us, event | category | flops | bytes accessed | tf_op | source)
XLA Modules:
  0.0 509.8 jit_solution(7640483992801324631)
XLA Ops:
  2.1 4.6 collective-permute-start
  10.5 4.2 all-to-all-start
  14.7 10.6 %reshape.184 = f32[8,2,8,2,64,2]{5,4,3,2,1,0:T(8,128)} reshape(f32[16,16,128]{2,1,0:T(8,128)} %param.7) | data formatting | bytes 262144 | tf_op jit(solution)/shard_map/reshape | solution.py:111
  25.3 4.0 reduce_sum.96
  30.0 4.2 collective-permute-start.24
  43.7 5.3 %collective-permute-start.4 = (f32[20,20,2]{2,1,0:T(8,128)S(1)}, f32[20,20,2]{2,1,0:T(8,128)S(1)}, u32[]{:S(2)}, u32[]{:S(2)}) collective-permute-start(f32[20,20,2]{2,1,0:T(8,128)S(1)} %get-tuple-element.29), channel_id=1, source_target_pairs={{0,1},{1,2},{2,3},{4,5},{5,6},{6,7},{8,9},{9,10},{10,11},{12,13},{... | collective-permute-start | bytes 9608 | tf_op jit(solution)/shard_map/ppermute | solution.py:20
  52.1 4.4 collective-permute-done.5
  58.6 4.3 collective-permute-start.6
  74.0 4.6 collective-permute-start.10
  81.4 4.4 collective-permute-done.11
  94.6 4.0 collective-permute-start.14
  103.3 4.0 collective-permute-start.16
  110.4 4.4 collective-permute-done.17
  117.0 4.3 collective-permute-start.18
  133.0 4.7 collective-permute-start.22
  140.6 4.4 collective-permute-done.23
  145.5 9.8 %reshape.183 = f32[8,2,8,2,64,2]{5,4,3,2,1,0:T(8,128)} reshape(f32[16,16,128]{2,1,0:T(8,128)S(1)} %fusion.55) | data formatting | bytes 262144 | tf_op jit(solution)/shard_map/reshape | solution.py:111
  155.2 4.1 reduce_sum.95
  159.4 4.3 collective-permute-start.30
  173.9 4.6 collective-permute-start.34
  180.5 3.8 collective-permute-done.35
  196.9 4.7 collective-permute-start.40
  203.5 3.8 collective-permute-done.41
  219.4 4.7 collective-permute-start.46
  230.0 3.3 collective-permute-start.48
  237.6 3.7 collective-permute-start.50
  245.8 6.5 %collective-permute-start.52 = (f32[10,10,1]{2,1,0:T(8,128)S(1)}, f32[10,10,1]{2,1,0:T(8,128)S(1)}, u32[]{:S(2)}, u32[]{:S(2)}) collective-permute-start(f32[10,10,1]{2,1,0:T(8,128)S(1)} %get-tuple-element.65), channel_id=1, source_target_pairs={{0,1},{1,2},{2,3},{4,5},{5,6},{6,7},{8,9},{9,10},{10,11},{12,13},{... | collective-permute-start | bytes 1208 | tf_op jit(solution)/shard_map/ppermute | solution.py:20
  254.3 3.8 collective-permute-done.53
  259.4 4.3 collective-permute-start.60
  275.3 4.8 collective-permute-start.64
  286.0 10.1 %all-reduce.1 = (f32[]{:T(128)}, f32[]{:T(128)}) all-reduce(f32[]{:T(128)} %get-tuple-element.8, f32[]{:T(128)} %get-tuple-element.7), channel_id=1, replica_groups=mesh['gx'=4,'gy'=2,'gz'=4] {'gy','gz'}, use_global_device_ids=true, to_apply=%region_6.7 | all-reduce | flops 2 | bytes 16 | tf_op jit(solution)/shard_map/psum | solution.py:120
  296.1 9.9 %all-reduce.3 = (f32[]{:T(128)}, f32[]{:T(128)}) all-reduce(f32[]{:T(128)} %get-tuple-element.11, f32[]{:T(128)} %get-tuple-element.12), channel_id=1, replica_groups=mesh['gx'=4,'gy'=2,'gz'=4] {'gx'}, use_global_device_ids=true, to_apply=%region_7.8 | all-reduce | flops 2 | bytes 16 | tf_op jit(solution)/shard_map/psum | solution.py:120
  319.8 7.6 %collective-permute-start.70 = (f32[6,6,1]{2,1,0:T(8,128)S(1)}, f32[6,6,1]{2,1,0:T(8,128)S(1)}, u32[]{:S(2)}, u32[]{:S(2)}) collective-permute-start(f32[6,6,1]{2,1,0:T(8,128)S(1)} %get-tuple-element.111), channel_id=1, source_target_pairs={{0,1},{1,2},{2,3},{4,5},{5,6},{6,7},{8,9},{9,10},{10,11},{12,13},{... | collective-permute-start | bytes 440 | tf_op jit(solution)/shard_map/ppermute | solution.py:20
  333.3 10.1 %all-reduce = (f32[]{:T(128)}, f32[]{:T(128)}) all-reduce(f32[]{:T(128)} %get-tuple-element.6, f32[]{:T(128)} %get-tuple-element.5), channel_id=1, replica_groups=mesh['gx'=4,'gy'=2,'gz'=4] {'gy','gz'}, use_global_device_ids=true, to_apply=%region_13.14 | all-reduce | flops 2 | bytes 16 | tf_op jit(solution)/shard_map/psum | solution.py:120
  343.5 7.8 %all-reduce.2 = (f32[]{:T(128)}, f32[]{:T(128)}) all-reduce(f32[]{:T(128)} %get-tuple-element.9, f32[]{:T(128)} %get-tuple-element.10), channel_id=1, replica_groups=mesh['gx'=4,'gy'=2,'gz'=4] {'gx'}, use_global_device_ids=true, to_apply=%region_14.15 | all-reduce | flops 2 | bytes 16 | tf_op jit(solution)/shard_map/psum | solution.py:120
  367.2 7.9 %collective-permute-start.76 = (f32[10,10,1]{2,1,0:T(8,128)S(1)}, f32[10,10,1]{2,1,0:T(8,128)S(1)}, u32[]{:S(2)}, u32[]{:S(2)}) collective-permute-start(f32[10,10,1]{2,1,0:T(8,128)S(1)} %get-tuple-element.63), channel_id=1, source_target_pairs={{0,1},{1,2},{2,3},{4,5},{5,6},{6,7},{8,9},{9,10},{10,11},{12,13},{... | collective-permute-start | bytes 1208 | tf_op jit(solution)/shard_map/ppermute | solution.py:20
  377.0 3.8 collective-permute-done.77
  392.8 4.7 collective-permute-start.82
  399.5 3.8 collective-permute-done.83
  416.4 4.7 collective-permute-start.88
  423.1 3.8 collective-permute-done.89
  438.9 4.7 collective-permute-start.94
  445.6 3.8 collective-permute-done.95
  466.1 4.7 collective-permute-start.100
  473.9 4.4 collective-permute-done.101
  490.4 3.2 collective-permute-done.105
  493.8 4.6 collective-permute-start.106
  501.6 4.4 collective-permute-done.107
  (364 shorter events, 258.6 us)
Async XLA Ops:
  0.8 35.1 %collective-permute-start.1 = (f32[2,16,128]{2,1,0:T(8,128)S(1)}, f32[2,16,128]{2,1,0:T(8,128)S(1)}, u32[]{:S(2)}, u32[]{:S(2)}) collective-permute-start(f32[2,16,128]{2,1,0:T(8,128)S(1)} %get-tuple-element.55), channel_id=1, source_target_pairs={{8,0},{16,8},{24,16},{9,1},{17,9},{25,17},{10,2},{18,10},{26,18},{... | collective-permute-start | bytes 49160 | tf_op jit(solution)/shard_map/ppermute | solution.py:22
  2.1 33.8 %collective-permute-start = (f32[2,16,128]{2,1,0:T(8,128)S(1)}, f32[2,16,128]{2,1,0:T(8,128)S(1)}, u32[]{:S(2)}, u32[]{:S(2)}) collective-permute-start(f32[2,16,128]{2,1,0:T(8,128)S(1)} %get-tuple-element.56), channel_id=1, source_target_pairs={{0,8},{8,16},{16,24},{1,9},{9,17},{17,25},{2,10},{10,18},{18,26},{... | collective-permute-start | bytes 49160 | tf_op jit(solution)/shard_map/ppermute | solution.py:20
  10.5 46.4 %all-to-all-start = ((bf16[4,2,4096]{2,1,0:T(2,128)(2,1)}), bf16[4,2,4096]{2,1,0:T(2,128)(2,1)S(1)}, u32[]{:S(2)}, u32[]{:S(2)}) async-start(bf16[4,2,4096]{2,1,0:T(2,128)(2,1)} %all_to_all.6), calls=%async_computation | async-start | bytes 131072 | tf_op jit(solution)/shard_map/all_to_all | solution.py:154
  30.0 61.0 %collective-permute-start.24 = (f32[1,8,64]{2,1,0:T(8,128)}, f32[1,8,64]{2,1,0:T(8,128)}, u32[]{:S(2)}, u32[]{:S(2)}) collective-permute-start(f32[1,8,64]{2,1,0:T(8,128)} %get-tuple-element.109), channel_id=1, source_target_pairs={{0,8},{8,16},{16,24},{1,9},{9,17},{17,25},{2,10},{10,18},{18,26},{... | collective-permute-start | bytes 6152 | tf_op jit(solution)/shard_map/ppermute | solution.py:20
  34.2 56.8 %collective-permute-start.25 = (f32[1,8,64]{2,1,0:T(8,128)}, f32[1,8,64]{2,1,0:T(8,128)}, u32[]{:S(2)}, u32[]{:S(2)}) collective-permute-start(f32[1,8,64]{2,1,0:T(8,128)} %get-tuple-element.110), channel_id=1, source_target_pairs={{8,0},{16,8},{24,16},{9,1},{17,9},{25,17},{10,2},{18,10},{26,18},{... | collective-permute-start | bytes 6152 | tf_op jit(solution)/shard_map/ppermute | solution.py:22
  43.7 8.4 %collective-permute-start.4 = (f32[20,20,2]{2,1,0:T(8,128)S(1)}, f32[20,20,2]{2,1,0:T(8,128)S(1)}, u32[]{:S(2)}, u32[]{:S(2)}) collective-permute-start(f32[20,20,2]{2,1,0:T(8,128)S(1)} %get-tuple-element.29), channel_id=1, source_target_pairs={{0,1},{1,2},{2,3},{4,5},{5,6},{6,7},{8,9},{9,10},{10,11},{12,13},{... | collective-permute-start | bytes 9608 | tf_op jit(solution)/shard_map/ppermute | solution.py:20
  49.0 7.5 %collective-permute-start.5 = (f32[20,20,2]{2,1,0:T(8,128)S(1)}, f32[20,20,2]{2,1,0:T(8,128)S(1)}, u32[]{:S(2)}, u32[]{:S(2)}) collective-permute-start(f32[20,20,2]{2,1,0:T(8,128)S(1)} %get-tuple-element.30), channel_id=1, source_target_pairs={{1,0},{2,1},{3,2},{5,4},{6,5},{7,6},{9,8},{10,9},{11,10},{13,12},{... | collective-permute-start | bytes 9608 | tf_op jit(solution)/shard_map/ppermute | solution.py:22
  58.6 6.3 %collective-permute-start.6 = (f32[1,16,128]{2,1,0:T(8,128)S(1)}, f32[1,16,128]{2,1,0:T(8,128)S(1)}, u32[]{:S(2)}, u32[]{:S(2)}) collective-permute-start(f32[1,16,128]{2,1,0:T(8,128)S(1)} %slice.1002), channel_id=1, source_target_pairs={{0,8},{8,16},{16,24},{1,9},{9,17},{17,25},{2,10},{10,18},{18,26},{... | collective-permute-start | bytes 24584 | tf_op jit(solution)/shard_map/ppermute | solution.py:20
  74.0 7.5 %collective-permute-start.10 = (f32[18,18,1]{2,1,0:T(8,128)S(1)}, f32[18,18,1]{2,1,0:T(8,128)S(1)}, u32[]{:S(2)}, u32[]{:S(2)}) collective-permute-start(f32[18,18,1]{2,1,0:T(8,128)S(1)} %get-tuple-element.33), channel_id=1, source_target_pairs={{0,1},{1,2},{2,3},{4,5},{5,6},{6,7},{8,9},{9,10},{10,11},{12,13},{... | collective-permute-start | bytes 3896 | tf_op jit(solution)/shard_map/ppermute | solution.py:20
  78.6 7.3 %collective-permute-start.11 = (f32[18,18,1]{2,1,0:T(8,128)S(1)}, f32[18,18,1]{2,1,0:T(8,128)S(1)}, u32[]{:S(2)}, u32[]{:S(2)}) collective-permute-start(f32[18,18,1]{2,1,0:T(8,128)S(1)} %get-tuple-element.34), channel_id=1, source_target_pairs={{1,0},{2,1},{3,2},{5,4},{6,5},{7,6},{9,8},{10,9},{11,10},{13,12},{... | collective-permute-start | bytes 3896 | tf_op jit(solution)/shard_map/ppermute | solution.py:22
  87.1 7.5 %collective-permute-start.12 = (f32[2,16,128]{2,1,0:T(8,128)S(1)}, f32[2,16,128]{2,1,0:T(8,128)S(1)}, u32[]{:S(2)}, u32[]{:S(2)}) collective-permute-start(f32[2,16,128]{2,1,0:T(8,128)S(1)} %get-tuple-element.53), channel_id=1, source_target_pairs={{0,8},{8,16},{16,24},{1,9},{9,17},{17,25},{2,10},{10,18},{18,26},{... | collective-permute-start | bytes 49160 | tf_op jit(solution)/shard_map/ppermute | solution.py:20
  91.9 17.4 %collective-permute-start.26 = (f32[10,1,64]{2,1,0:T(1,128)S(1)}, f32[10,1,64]{2,1,0:T(1,128)S(1)}, u32[]{:S(2)}, u32[]{:S(2)}) collective-permute-start(f32[10,1,64]{2,1,0:T(1,128)S(1)} %get-tuple-element.91), channel_id=1, source_target_pairs={{0,4},{1,5},{2,6},{3,7},{8,12},{9,13},{10,14},{11,15},{16,20},{17,... | collective-permute-start | bytes 7688 | tf_op jit(solution)/shard_map/ppermute | solution.py:20
  93.3 16.0 %collective-permute-start.27 = (f32[10,1,64]{2,1,0:T(1,128)S(1)}, f32[10,1,64]{2,1,0:T(1,128)S(1)}, u32[]{:S(2)}, u32[]{:S(2)}) collective-permute-start(f32[10,1,64]{2,1,0:T(1,128)S(1)} %get-tuple-element.92), channel_id=1, source_target_pairs={{4,0},{5,1},{6,2},{7,3},{12,8},{13,9},{14,10},{15,11},{20,16},{21,... | collective-permute-start | bytes 7688 | tf_op jit(solution)/shard_map/ppermute | solution.py:22
  94.6 6.1 %collective-permute-start.14 = (f32[20,2,128]{2,1,0:T(2,128)S(1)}, f32[20,2,128]{2,1,0:T(2,128)S(1)}, u32[]{:S(2)}, u32[]{:S(2)}) collective-permute-start(f32[20,2,128]{2,1,0:T(2,128)S(1)} %get-tuple-element.39), channel_id=1, source_target_pairs={{0,4},{1,5},{2,6},{3,7},{8,12},{9,13},{10,14},{11,15},{16,20},{17,... | collective-permute-start | bytes 61448 | tf_op jit(solution)/shard_map/ppermute | solution.py:20
  103.3 7.1 %collective-permute-start.16 = (f32[20,20,2]{2,1,0:T(8,128)S(1)}, f32[20,20,2]{2,1,0:T(8,128)S(1)}, u32[]{:S(2)}, u32[]{:S(2)}) collective-permute-start(f32[20,20,2]{2,1,0:T(8,128)S(1)} %get-tuple-element.27), channel_id=1, source_target_pairs={{0,1},{1,2},{2,3},{4,5},{5,6},{6,7},{8,9},{9,10},{10,11},{12,13},{... | collective-permute-start | bytes 9608 | tf_op jit(solution)/shard_map/ppermute | solution.py:20
  107.3 7.5 %collective-permute-start.17 = (f32[20,20,2]{2,1,0:T(8,128)S(1)}, f32[20,20,2]{2,1,0:T(8,128)S(1)}, u32[]{:S(2)}, u32[]{:S(2)}) collective-permute-start(f32[20,20,2]{2,1,0:T(8,128)S(1)} %get-tuple-element.28), channel_id=1, source_target_pairs={{1,0},{2,1},{3,2},{5,4},{6,5},{7,6},{9,8},{10,9},{11,10},{13,12},{... | collective-permute-start | bytes 9608 | tf_op jit(solution)/shard_map/ppermute | solution.py:22
  117.0 10.0 %collective-permute-start.18 = (f32[1,16,128]{2,1,0:T(8,128)S(1)}, f32[1,16,128]{2,1,0:T(8,128)S(1)}, u32[]{:S(2)}, u32[]{:S(2)}) collective-permute-start(f32[1,16,128]{2,1,0:T(8,128)S(1)} %get-tuple-element.51), channel_id=1, source_target_pairs={{0,8},{8,16},{16,24},{1,9},{9,17},{17,25},{2,10},{10,18},{18,26},{... | collective-permute-start | bytes 24584 | tf_op jit(solution)/shard_map/ppermute | solution.py:20
  122.7 17.1 %collective-permute-start.28 = (f32[10,10,1]{2,1,0:T(8,128)S(1)}, f32[10,10,1]{2,1,0:T(8,128)S(1)}, u32[]{:S(2)}, u32[]{:S(2)}) collective-permute-start(f32[10,10,1]{2,1,0:T(8,128)S(1)} %get-tuple-element.73), channel_id=1, source_target_pairs={{0,1},{1,2},{2,3},{4,5},{5,6},{6,7},{8,9},{9,10},{10,11},{12,13},{... | collective-permute-start | bytes 1208 | tf_op jit(solution)/shard_map/ppermute | solution.py:20
  124.7 15.1 %collective-permute-start.29 = (f32[10,10,1]{2,1,0:T(8,128)S(1)}, f32[10,10,1]{2,1,0:T(8,128)S(1)}, u32[]{:S(2)}, u32[]{:S(2)}) collective-permute-start(f32[10,10,1]{2,1,0:T(8,128)S(1)} %get-tuple-element.74), channel_id=1, source_target_pairs={{1,0},{2,1},{3,2},{5,4},{6,5},{7,6},{9,8},{10,9},{11,10},{13,12},{... | collective-permute-start | bytes 1208 | tf_op jit(solution)/shard_map/ppermute | solution.py:22
  133.0 7.6 %collective-permute-start.22 = (f32[18,18,1]{2,1,0:T(8,128)S(1)}, f32[18,18,1]{2,1,0:T(8,128)S(1)}, u32[]{:S(2)}, u32[]{:S(2)}) collective-permute-start(f32[18,18,1]{2,1,0:T(8,128)S(1)} %get-tuple-element.31), channel_id=1, source_target_pairs={{0,1},{1,2},{2,3},{4,5},{5,6},{6,7},{8,9},{9,10},{10,11},{12,13},{... | collective-permute-start | bytes 3896 | tf_op jit(solution)/shard_map/ppermute | solution.py:20
  137.7 7.3 %collective-permute-start.23 = (f32[18,18,1]{2,1,0:T(8,128)S(1)}, f32[18,18,1]{2,1,0:T(8,128)S(1)}, u32[]{:S(2)}, u32[]{:S(2)}) collective-permute-start(f32[18,18,1]{2,1,0:T(8,128)S(1)} %get-tuple-element.32), channel_id=1, source_target_pairs={{1,0},{2,1},{3,2},{5,4},{6,5},{7,6},{9,8},{10,9},{11,10},{13,12},{... | collective-permute-start | bytes 3896 | tf_op jit(solution)/shard_map/ppermute | solution.py:22
  173.9 6.5 %collective-permute-start.34 = (f32[10,10,1]{2,1,0:T(8,128)S(1)}, f32[10,10,1]{2,1,0:T(8,128)S(1)}, u32[]{:S(2)}, u32[]{:S(2)}) collective-permute-start(f32[10,10,1]{2,1,0:T(8,128)S(1)} %get-tuple-element.71), channel_id=1, source_target_pairs={{0,1},{1,2},{2,3},{4,5},{5,6},{6,7},{8,9},{9,10},{10,11},{12,13},{... | collective-permute-start | bytes 1208 | tf_op jit(solution)/shard_map/ppermute | solution.py:20
  178.5 5.8 %collective-permute-start.35 = (f32[10,10,1]{2,1,0:T(8,128)S(1)}, f32[10,10,1]{2,1,0:T(8,128)S(1)}, u32[]{:S(2)}, u32[]{:S(2)}) collective-permute-start(f32[10,10,1]{2,1,0:T(8,128)S(1)} %get-tuple-element.72), channel_id=1, source_target_pairs={{1,0},{2,1},{3,2},{5,4},{6,5},{7,6},{9,8},{10,9},{11,10},{13,12},{... | collective-permute-start | bytes 1208 | tf_op jit(solution)/shard_map/ppermute | solution.py:22
  196.9 6.6 %collective-permute-start.40 = (f32[10,10,1]{2,1,0:T(8,128)S(1)}, f32[10,10,1]{2,1,0:T(8,128)S(1)}, u32[]{:S(2)}, u32[]{:S(2)}) collective-permute-start(f32[10,10,1]{2,1,0:T(8,128)S(1)} %get-tuple-element.69), channel_id=1, source_target_pairs={{0,1},{1,2},{2,3},{4,5},{5,6},{6,7},{8,9},{9,10},{10,11},{12,13},{... | collective-permute-start | bytes 1208 | tf_op jit(solution)/shard_map/ppermute | solution.py:20
  201.6 5.8 %collective-permute-start.41 = (f32[10,10,1]{2,1,0:T(8,128)S(1)}, f32[10,10,1]{2,1,0:T(8,128)S(1)}, u32[]{:S(2)}, u32[]{:S(2)}) collective-permute-start(f32[10,10,1]{2,1,0:T(8,128)S(1)} %get-tuple-element.70), channel_id=1, source_target_pairs={{1,0},{2,1},{3,2},{5,4},{6,5},{7,6},{9,8},{10,9},{11,10},{13,12},{... | collective-permute-start | bytes 1208 | tf_op jit(solution)/shard_map/ppermute | solution.py:22
  219.4 9.7 %collective-permute-start.46 = (f32[10,10,1]{2,1,0:T(8,128)S(1)}, f32[10,10,1]{2,1,0:T(8,128)S(1)}, u32[]{:S(2)}, u32[]{:S(2)}) collective-permute-start(f32[10,10,1]{2,1,0:T(8,128)S(1)} %get-tuple-element.67), channel_id=1, source_target_pairs={{0,1},{1,2},{2,3},{4,5},{5,6},{6,7},{8,9},{9,10},{10,11},{12,13},{... | collective-permute-start | bytes 1208 | tf_op jit(solution)/shard_map/ppermute | solution.py:20
  224.1 5.8 %collective-permute-start.47 = (f32[10,10,1]{2,1,0:T(8,128)S(1)}, f32[10,10,1]{2,1,0:T(8,128)S(1)}, u32[]{:S(2)}, u32[]{:S(2)}) collective-permute-start(f32[10,10,1]{2,1,0:T(8,128)S(1)} %get-tuple-element.68), channel_id=1, source_target_pairs={{1,0},{2,1},{3,2},{5,4},{6,5},{7,6},{9,8},{10,9},{11,10},{13,12},{... | collective-permute-start | bytes 1208 | tf_op jit(solution)/shard_map/ppermute | solution.py:22
  226.0 8.6 %collective-permute-start.54 = (f32[1,4,32]{2,1,0:T(4,128)S(1)}, f32[1,4,32]{2,1,0:T(4,128)S(1)}, u32[]{:S(2)}, u32[]{:S(2)}) collective-permute-start(f32[1,4,32]{2,1,0:T(4,128)S(1)} %get-tuple-element.125), channel_id=1, source_target_pairs={{0,8},{8,16},{16,24},{1,9},{9,17},{17,25},{2,10},{10,18},{18,26},{... | collective-permute-start | bytes 1544 | tf_op jit(solution)/shard_map/ppermute | solution.py:20
  227.7 6.9 %collective-permute-start.55 = (f32[1,4,32]{2,1,0:T(4,128)S(1)}, f32[1,4,32]{2,1,0:T(4,128)S(1)}, u32[]{:S(2)}, u32[]{:S(2)}) collective-permute-start(f32[1,4,32]{2,1,0:T(4,128)S(1)} %get-tuple-element.126), channel_id=1, source_target_pairs={{8,0},{16,8},{24,16},{9,1},{17,9},{25,17},{10,2},{18,10},{26,18},{... | collective-permute-start | bytes 1544 | tf_op jit(solution)/shard_map/ppermute | solution.py:22
  230.0 7.3 %collective-permute-start.48 = (f32[1,8,64]{2,1,0:T(8,128)S(1)}, f32[1,8,64]{2,1,0:T(8,128)S(1)}, u32[]{:S(2)}, u32[]{:S(2)}) collective-permute-start(f32[1,8,64]{2,1,0:T(8,128)S(1)} %get-tuple-element.101), channel_id=1, source_target_pairs={{0,8},{8,16},{16,24},{1,9},{9,17},{17,25},{2,10},{10,18},{18,26},{... | collective-permute-start | bytes 6152 | tf_op jit(solution)/shard_map/ppermute | solution.py:20
  234.6 19.6 %collective-permute-start.56 = (f32[6,1,32]{2,1,0:T(1,128)S(1)}, f32[6,1,32]{2,1,0:T(1,128)S(1)}, u32[]{:S(2)}, u32[]{:S(2)}) collective-permute-start(f32[6,1,32]{2,1,0:T(1,128)S(1)} %get-tuple-element.119), channel_id=1, source_target_pairs={{0,4},{1,5},{2,6},{3,7},{8,12},{9,13},{10,14},{11,15},{16,20},{17,... | collective-permute-start | bytes 2312 | tf_op jit(solution)/shard_map/ppermute | solution.py:20
  236.0 18.2 %collective-permute-start.57 = (f32[6,1,32]{2,1,0:T(1,128)S(1)}, f32[6,1,32]{2,1,0:T(1,128)S(1)}, u32[]{:S(2)}, u32[]{:S(2)}) collective-permute-start(f32[6,1,32]{2,1,0:T(1,128)S(1)} %get-tuple-element.120), channel_id=1, source_target_pairs={{4,0},{5,1},{6,2},{7,3},{12,8},{13,9},{14,10},{15,11},{20,16},{21,... | collective-permute-start | bytes 2312 | tf_op jit(solution)/shard_map/ppermute | solution.py:22
  245.8 8.5 %collective-permute-start.52 = (f32[10,10,1]{2,1,0:T(8,128)S(1)}, f32[10,10,1]{2,1,0:T(8,128)S(1)}, u32[]{:S(2)}, u32[]{:S(2)}) collective-permute-start(f32[10,10,1]{2,1,0:T(8,128)S(1)} %get-tuple-element.65), channel_id=1, source_target_pairs={{0,1},{1,2},{2,3},{4,5},{5,6},{6,7},{8,9},{9,10},{10,11},{12,13},{... | collective-permute-start | bytes 1208 | tf_op jit(solution)/shard_map/ppermute | solution.py:20
  252.3 5.8 %collective-permute-start.53 = (f32[10,10,1]{2,1,0:T(8,128)S(1)}, f32[10,10,1]{2,1,0:T(8,128)S(1)}, u32[]{:S(2)}, u32[]{:S(2)}) collective-permute-start(f32[10,10,1]{2,1,0:T(8,128)S(1)} %get-tuple-element.66), channel_id=1, source_target_pairs={{1,0},{2,1},{3,2},{5,4},{6,5},{7,6},{9,8},{10,9},{11,10},{13,12},{... | collective-permute-start | bytes 1208 | tf_op jit(solution)/shard_map/ppermute | solution.py:22
  259.4 10.0 %collective-permute-start.60 = (f32[1,4,32]{2,1,0:T(4,128)S(1)}, f32[1,4,32]{2,1,0:T(4,128)S(1)}, u32[]{:S(2)}, u32[]{:S(2)}) collective-permute-start(f32[1,4,32]{2,1,0:T(4,128)S(1)} %get-tuple-element.127), channel_id=1, source_target_pairs={{0,8},{8,16},{16,24},{1,9},{9,17},{17,25},{2,10},{10,18},{18,26},{... | collective-permute-start | bytes 1544 | tf_op jit(solution)/shard_map/ppermute | solution.py:20
  265.1 16.9 %collective-permute-start.58 = (f32[6,6,1]{2,1,0:T(8,128)S(1)}, f32[6,6,1]{2,1,0:T(8,128)S(1)}, u32[]{:S(2)}, u32[]{:S(2)}) collective-permute-start(f32[6,6,1]{2,1,0:T(8,128)S(1)} %get-tuple-element.113), channel_id=1, source_target_pairs={{0,1},{1,2},{2,3},{4,5},{5,6},{6,7},{8,9},{9,10},{10,11},{12,13},{... | collective-permute-start | bytes 440 | tf_op jit(solution)/shard_map/ppermute | solution.py:20
  267.2 14.8 %collective-permute-start.59 = (f32[6,6,1]{2,1,0:T(8,128)S(1)}, f32[6,6,1]{2,1,0:T(8,128)S(1)}, u32[]{:S(2)}, u32[]{:S(2)}) collective-permute-start(f32[6,6,1]{2,1,0:T(8,128)S(1)} %get-tuple-element.114), channel_id=1, source_target_pairs={{1,0},{2,1},{3,2},{5,4},{6,5},{7,6},{9,8},{10,9},{11,10},{13,12},{... | collective-permute-start | bytes 440 | tf_op jit(solution)/shard_map/ppermute | solution.py:22
  275.3 7.6 %collective-permute-start.64 = (f32[6,6,1]{2,1,0:T(8,128)S(1)}, f32[6,6,1]{2,1,0:T(8,128)S(1)}, u32[]{:S(2)}, u32[]{:S(2)}) collective-permute-start(f32[6,6,1]{2,1,0:T(8,128)S(1)} %get-tuple-element.115), channel_id=1, source_target_pairs={{0,1},{1,2},{2,3},{4,5},{5,6},{6,7},{8,9},{9,10},{10,11},{12,13},{... | collective-permute-start | bytes 440 | tf_op jit(solution)/shard_map/ppermute | solution.py:20
  319.8 9.5 %collective-permute-start.70 = (f32[6,6,1]{2,1,0:T(8,128)S(1)}, f32[6,6,1]{2,1,0:T(8,128)S(1)}, u32[]{:S(2)}, u32[]{:S(2)}) collective-permute-start(f32[6,6,1]{2,1,0:T(8,128)S(1)} %get-tuple-element.111), channel_id=1, source_target_pairs={{0,1},{1,2},{2,3},{4,5},{5,6},{6,7},{8,9},{9,10},{10,11},{12,13},{... | collective-permute-start | bytes 440 | tf_op jit(solution)/shard_map/ppermute | solution.py:20
  367.2 9.8 %collective-permute-start.76 = (f32[10,10,1]{2,1,0:T(8,128)S(1)}, f32[10,10,1]{2,1,0:T(8,128)S(1)}, u32[]{:S(2)}, u32[]{:S(2)}) collective-permute-start(f32[10,10,1]{2,1,0:T(8,128)S(1)} %get-tuple-element.63), channel_id=1, source_target_pairs={{0,1},{1,2},{2,3},{4,5},{5,6},{6,7},{8,9},{9,10},{10,11},{12,13},{... | collective-permute-start | bytes 1208 | tf_op jit(solution)/shard_map/ppermute | solution.py:20
  375.0 5.8 %collective-permute-start.77 = (f32[10,10,1]{2,1,0:T(8,128)S(1)}, f32[10,10,1]{2,1,0:T(8,128)S(1)}, u32[]{:S(2)}, u32[]{:S(2)}) collective-permute-start(f32[10,10,1]{2,1,0:T(8,128)S(1)} %get-tuple-element.64), channel_id=1, source_target_pairs={{1,0},{2,1},{3,2},{5,4},{6,5},{7,6},{9,8},{10,9},{11,10},{13,12},{... | collective-permute-start | bytes 1208 | tf_op jit(solution)/shard_map/ppermute | solution.py:22
  392.8 6.6 %collective-permute-start.82 = (f32[10,10,1]{2,1,0:T(8,128)S(1)}, f32[10,10,1]{2,1,0:T(8,128)S(1)}, u32[]{:S(2)}, u32[]{:S(2)}) collective-permute-start(f32[10,10,1]{2,1,0:T(8,128)S(1)} %get-tuple-element.61), channel_id=1, source_target_pairs={{0,1},{1,2},{2,3},{4,5},{5,6},{6,7},{8,9},{9,10},{10,11},{12,13},{... | collective-permute-start | bytes 1208 | tf_op jit(solution)/shard_map/ppermute | solution.py:20
  416.4 6.6 %collective-permute-start.88 = (f32[10,10,1]{2,1,0:T(8,128)S(1)}, f32[10,10,1]{2,1,0:T(8,128)S(1)}, u32[]{:S(2)}, u32[]{:S(2)}) collective-permute-start(f32[10,10,1]{2,1,0:T(8,128)S(1)} %get-tuple-element.59), channel_id=1, source_target_pairs={{0,1},{1,2},{2,3},{4,5},{5,6},{6,7},{8,9},{9,10},{10,11},{12,13},{... | collective-permute-start | bytes 1208 | tf_op jit(solution)/shard_map/ppermute | solution.py:20
  438.9 6.6 %collective-permute-start.94 = (f32[10,10,1]{2,1,0:T(8,128)S(1)}, f32[10,10,1]{2,1,0:T(8,128)S(1)}, u32[]{:S(2)}, u32[]{:S(2)}) collective-permute-start(f32[10,10,1]{2,1,0:T(8,128)S(1)} %get-tuple-element.57), channel_id=1, source_target_pairs={{0,1},{1,2},{2,3},{4,5},{5,6},{6,7},{8,9},{9,10},{10,11},{12,13},{... | collective-permute-start | bytes 1208 | tf_op jit(solution)/shard_map/ppermute | solution.py:20
  466.1 7.8 %collective-permute-start.100 = (f32[20,20,2]{2,1,0:T(8,128)S(1)}, f32[20,20,2]{2,1,0:T(8,128)S(1)}, u32[]{:S(2)}, u32[]{:S(2)}) collective-permute-start(f32[20,20,2]{2,1,0:T(8,128)S(1)} %get-tuple-element.25), channel_id=1, source_target_pairs={{0,1},{1,2},{2,3},{4,5},{5,6},{6,7},{8,9},{9,10},{10,11},{12,13},{... | collective-permute-start | bytes 9608 | tf_op jit(solution)/shard_map/ppermute | solution.py:20
  470.8 7.5 %collective-permute-start.101 = (f32[20,20,2]{2,1,0:T(8,128)S(1)}, f32[20,20,2]{2,1,0:T(8,128)S(1)}, u32[]{:S(2)}, u32[]{:S(2)}) collective-permute-start(f32[20,20,2]{2,1,0:T(8,128)S(1)} %get-tuple-element.26), channel_id=1, source_target_pairs={{1,0},{2,1},{3,2},{5,4},{6,5},{7,6},{9,8},{10,9},{11,10},{13,12},{... | collective-permute-start | bytes 9608 | tf_op jit(solution)/shard_map/ppermute | solution.py:22
  493.8 7.7 %collective-permute-start.106 = (f32[20,20,2]{2,1,0:T(8,128)S(1)}, f32[20,20,2]{2,1,0:T(8,128)S(1)}, u32[]{:S(2)}, u32[]{:S(2)}) collective-permute-start(f32[20,20,2]{2,1,0:T(8,128)S(1)} %get-tuple-element.23), channel_id=1, source_target_pairs={{0,1},{1,2},{2,3},{4,5},{5,6},{6,7},{8,9},{9,10},{10,11},{12,13},{... | collective-permute-start | bytes 9608 | tf_op jit(solution)/shard_map/ppermute | solution.py:20
  498.4 7.5 %collective-permute-start.107 = (f32[20,20,2]{2,1,0:T(8,128)S(1)}, f32[20,20,2]{2,1,0:T(8,128)S(1)}, u32[]{:S(2)}, u32[]{:S(2)}) collective-permute-start(f32[20,20,2]{2,1,0:T(8,128)S(1)} %get-tuple-element.24), channel_id=1, source_target_pairs={{1,0},{2,1},{3,2},{5,4},{6,5},{7,6},{9,8},{10,9},{11,10},{13,12},{... | collective-permute-start | bytes 9608 | tf_op jit(solution)/shard_map/ppermute | solution.py:22
  (78 other events, 1086.5 us)
